TPU v7x, 32 devices: a whole 2x2x4 slice. The times are simulated.
32 devices in a mesh: pts: 4 (over y, x), med: 8 (over z, core).
Axes of the slice: x: 2, y: 2, z: 4, core: 2. Of those that a mesh axis runs over, the one named last changes fastest.
Arguments:
- points: float32 [65536, 1024], P(('pts', 'med')), may hold values from -6 to 6
- weights: float32 [65536], P(('pts', 'med')), may hold values from 0.2 to 6
- medoid_ids: int32 [512], replicated, may hold values from 0 to 65535, as said below
Outputs:
- cover: float32 [65536], P(('pts', 'med'))
- total: float32 [], replicated
Inputs may be any that keep to these rules, and one draw needn't show every extreme that they name: `medoid_ids`: distinct row numbers; the points of one device hold at most 24 medoids, and some device holds exactly 24 in every draw.
All inputs are finite; a program needn't handle non-finite values.
Results may differ from a plain program's by a relative error of at most 0.00005.
Values sent between devices are 32-bit elements; how exact they have to be, the bound alone decides.
A program may use at most 128 MiB of HBM per device.

v0:
```python
import jax
import jax.numpy as jnp
from jax import lax
from jax.sharding import PartitionSpec as P

MED_DEV = 16
EPS = 1e-06


def best_match(unit, block, offset):
    sims = lax.dot_general(
        unit,
        block,
        (((1,), (1,)), ((), ())),
        precision=lax.Precision.HIGHEST,
        preferred_element_type=jnp.float32,
    )
    return jnp.max(sims + offset[None, :], axis=1)


def slot_offsets(counts, global_rows, group_pts, group_med, capacity):
    group_rows = group_pts * capacity
    med_of = global_rows // group_rows
    within = global_rows % group_rows
    pts_of = within // capacity
    slot_of = within % capacity
    device_of = pts_of * group_med + med_of
    devices = jnp.arange(group_pts * group_med, dtype=jnp.int32)
    owned_count = jnp.sum(
        jnp.where(device_of[:, None] == devices[None, :], counts[None, :], 0), axis=1
    )
    return jnp.where(slot_of < owned_count, 0.0, -4.0).astype(jnp.float32)


def body(points, weights, medoid_ids):
    rows = points.shape[0]
    capacity = MED_DEV + MED_DEV // 2
    group_pts = lax.axis_size("pts")
    group_med = lax.axis_size("med")
    unit = points * lax.rsqrt(jnp.sum(points * points, axis=1, keepdims=True) + EPS)
    med_index = lax.axis_index("med")
    row_start = (lax.axis_index("pts") * group_med + med_index) * rows
    local = medoid_ids - row_start
    owned = jnp.logical_and(local >= 0, local < rows).astype(jnp.int32)
    rank = jnp.cumsum(owned) - 1
    slot_ids = jnp.arange(capacity, dtype=jnp.int32)
    select = jnp.logical_and(owned[None, :] == 1, rank[None, :] == slot_ids[:, None]).astype(
        jnp.int32
    )
    position = jnp.sum(select * local[None, :], axis=1)
    valid = jnp.sum(select, axis=1) > 0
    mine = jnp.take(unit, position, axis=0) * valid[:, None].astype(jnp.float32)
    owner_of = medoid_ids // rows
    devices = jnp.arange(group_pts * group_med, dtype=jnp.int32)
    counts = jnp.sum((owner_of[None, :] == devices[:, None]).astype(jnp.int32), axis=1)
    block = lax.all_gather(mine, "pts", axis=0, tiled=True)
    start_best = jnp.full((rows,), -8.0, jnp.float32)
    piece = lax.all_gather(block, "med", axis=0, tiled=True)
    global_rows = jnp.arange(piece.shape[0], dtype=jnp.int32)
    piece_offset = slot_offsets(counts, global_rows, group_pts, group_med, capacity)
    cover = jnp.maximum(start_best, best_match(unit, piece, piece_offset))
    both_sums = lax.psum(jnp.stack([jnp.sum(weights * cover), jnp.sum(weights)]), ("pts", "med"))
    return (cover, both_sums[0] / both_sums[1])


def solution(mesh):
    return jax.shard_map(
        body,
        mesh=mesh,
        in_specs=(P(("pts", "med"), None), P(("pts", "med")), P()),
        out_specs=(P(("pts", "med")), P()),
        check_vma=False,
    )
```

profile of v0, /device:TPU:0, one launch (start us, length us, event | category | flops | bytes accessed | tf_op | source)
XLA Modules:
  0.0 147.5 jit_solution(15723708422780872622)
XLA Ops:
  7.2 0.0 all-gather.2.cloned.1.call-start
  7.2 0.7 convert_compare_fusion
  7.9 0.3 reduce-window.9
  8.2 0.1 slice.13
  8.3 0.1 slice_reduce_fusion
  8.4 0.1 add_bitcast_fusion
  8.5 0.1 convert_reduce_fusion.1
  8.7 4.1 %multiply_reduce_fusion = f32[2048]{0:T(1024)S(1)} fusion(f32[2048,1024]{1,0:T(8,128)} %param.3), kind=kLoop, calls=%fused_computation.1 | loop fusion | flops 4192256 | bytes 8396800 | tf_op jit(solution)/shard_map/reduce_sum | solution.py:40
  12.9 1.2 copy-done
  14.1 3.8 %broadcast_multiply_fusion = f32[2048,1024]{1,0:T(8,128)} fusion(f32[2048,1024]{1,0:T(8,128)S(1)} %copy-done, f32[2048]{0:T(1024)S(1)} %add_rsqrt_fusion), kind=kLoop, calls=%fused_computation.3 | loop fusion | flops 2097152 | bytes 16785408 | tf_op jit(solution)/shard_map/mul | solution.py:40
  17.9 4.0 %gather_fusion = f32[24,1024]{1,0:T(8,128)S(1)} fusion(f32[2048,1024]{1,0:T(8,128)} %broadcast_multiply_fusion, s32[1024]{0:T(1024)S(1)} %pad_clamp_fusion), kind=kCustom, calls=%fused_computation | custom fusion | bytes 196704 | tf_op jit(solution)/shard_map/jit(_take)/gather | solution.py:52
  22.0 0.1 select_multiply_fusion
  22.0 11.7 %all_gather.6 = f32[96,1024]{1,0:T(8,128)} all-gather(f32[24,1024]{1,0:T(8,128)S(1)} %select_multiply_fusion), channel_id=1, replica_groups=mesh['pts'=4,'med'=8] {'pts'}, dimensions={0}, use_global_device_ids=true | all-gather | bytes 491520 | tf_op jit(solution)/shard_map/all_gather | solution.py:56
  33.7 0.0 all-gather.2.cloned.1.call-update
  33.8 0.0 copy-done.2
  33.8 0.1 convert_reduce_fusion
  33.9 0.1 select_reduce_fusion
  34.1 0.0 copy-start.1
  34.1 38.3 %all-gather.2.cloned.1.call-done = f32[768,1024]{1,0:T(8,128)} async-done(((f32[96,1024]{1,0:T(8,128)}), f32[768,1024]{1,0:T(8,128)}) %all-gather.2.cloned.1.call-update) | async-done | bytes 3145744 | tf_op jit(solution)/shard_map/all_gather | solution.py:58
  72.4 23.2 %add_reduce_fusion = f32[2048]{0:T(1024)S(1)} fusion(f32[2048,1024]{1,0:T(8,128)} %broadcast_multiply_fusion, f32[768,1024]{1,0:T(8,128)} %all-gather.2.cloned.1.call-done, f32[768]{0:T(1024)S(1)} %fusion.14), kind=kOutput, calls=%fused_computation.2 | convolution fusion | flops 19330496512 | bytes 11545600 | tf_op jit(solution)/shard_map/dot_general | solution.py:11
  95.7 1.3 multiply_reduce_fusion.1
  97.0 1.4 pad_maximum_fusion
  98.4 39.2 %psum.7 = f32[2]{0:T(128)S(1)} all-reduce(f32[2]{0:T(128)S(1)} %pad_maximum_fusion), channel_id=1, replica_groups=mesh['pts'=4,'med'=8] {'pts','med'}, use_global_device_ids=true, to_apply=%region_10.11 | all-reduce | flops 2 | bytes 16 | tf_op jit(solution)/shard_map/psum | solution.py:62
  137.5 0.6 fusion.18
  (12 shorter events, 0.1 us)
Async XLA Ops:
  7.2 65.2 %all-gather.2.cloned.1.call-start = ((), (), s32[]{:S(2)}) async-start(), calls=%async_computation | async-start | bytes 3538944 | tf_op jit(solution)/shard_map/all_gather | solution.py:58
  8.3 5.8 %copy-start = (f32[2048,1024]{1,0:T(8,128)S(1)}, f32[2048,1024]{1,0:T(8,128)}, u32[]{:S(2)}) copy-start(f32[2048,1024]{1,0:T(8,128)} %param.3) | copy-start | bytes 25165828
  14.1 19.7 %copy-start.2 = (s32[512]{0:T(512)S(1)}, s32[512]{0:T(512)}, u32[]{:S(2)}) copy-start(s32[512]{0:T(512)} %param.5) | copy-start | bytes 6148
  34.1 61.6 %copy-start.1 = (f32[2048]{0:T(1024)S(1)}, f32[2048]{0:T(1024)}, u32[]{:S(2)}) copy-start(f32[2048]{0:T(1024)} %param.4) | copy-start | bytes 24580
Sparse Core Ops, SparseCore 0:
  33.9 38.4 all-gather.1
where the time goes:
time: 148 us; the launch traced here: 147 us
  blocking collectives  50.9 us (34%)
  waiting for transfers between devices  38.4 us (26%)
  matrix products  23.2 us (16%)
  between operations  16.6 us (11%)
  other arithmetic  12.3 us (8%)
  local copies, waits for them, and re-layouts  6.06 us (4%)
    psum x1, blocking collectives, body(): lax.psum(jnp.stack([jnp.sum(weights * cover), jnp.sum(weights)]), ('pts',...  39.2 us
    all_gather x1, waiting for transfers between devices, body(): piece = lax.all_gather(block, 'med', axis=0, tiled=True)  38.3 us
    dot_general x1, matrix products, best_match(): lax.dot_general(unit, block, (((1,), (1,)), ((), ())), precision=lax.Prec...  23.2 us
    all_gather x1, blocking collectives, body(): block = lax.all_gather(mine, 'pts', axis=0, tiled=True)  11.7 us
    reduce_sum x1, other arithmetic, body(): jnp.sum(points * points, axis=1, keepdims=True) + EPS  4.15 us
    gather x1, local copies, waits for them, and re-layouts, body(): mine = jnp.take(unit, position, axis=0) * valid[:, None].astype(jnp.float32)  4.02 us
    mul x1, other arithmetic, body(): points * lax.rsqrt(jnp.sum(points * points, axis=1, keepdims=True) + EPS)  3.83 us
  transfers between devices with their start and end apart: 1, of which 1 were waited for; matrix products, arithmetic and copies ran while one was open for 0% of the time, Pallas kernels for 0%

commit v1 on v0

--- a/solution.py
+++ b/solution.py
@@ -5,6 +5,11 @@
 
 MED_DEV = 16
 EPS = 1e-06
+
+
+def gather_and_add(x, mesh_axis):
+    parts = lax.all_gather(x, mesh_axis)
+    return jnp.sum(parts, axis=0)
 
 
 def best_match(unit, block, offset):
@@ -59,7 +64,9 @@
     global_rows = jnp.arange(piece.shape[0], dtype=jnp.int32)
     piece_offset = slot_offsets(counts, global_rows, group_pts, group_med, capacity)
     cover = jnp.maximum(start_best, best_match(unit, piece, piece_offset))
-    both_sums = lax.psum(jnp.stack([jnp.sum(weights * cover), jnp.sum(weights)]), ("pts", "med"))
+    both_sums = gather_and_add(
+        jnp.stack([jnp.sum(weights * cover), jnp.sum(weights)]), ("pts", "med")
+    )
     return (cover, both_sums[0] / both_sums[1])
 
 

time: 148 us -> 148 us (level)
    psum x1 -> x0, blocking collectives: 39.2 us -> none  [body(): lax.psum(jnp.stack([jnp.sum(weights * cover), jnp.sum(weights)]), ('pts',...]
    unnamed x0 -> x1, blocking collectives: none -> 39.2 us
    unnamed x0 -> x1, other arithmetic: none -> 1.5 us
where the time goes in v1:
time: 148 us
  blocking collectives  50.9 us (34%)
  waiting for transfers between devices  38.4 us (26%)
  matrix products  23.3 us (16%)
  between operations  16.7 us (11%)
  other arithmetic  12.4 us (8%)
  local copies, waits for them, and re-layouts  6.16 us (4%)
    unnamed x1, blocking collectives  39.2 us
    all_gather x1, waiting for transfers between devices, body(): piece = lax.all_gather(block, 'med', axis=0, tiled=True)  38.3 us
    dot_general x1, matrix products, best_match(): lax.dot_general(unit, block, (((1,), (1,)), ((), ())), precision=lax.Prec...  23.3 us
    all_gather x1, blocking collectives, body(): block = lax.all_gather(mine, 'pts', axis=0, tiled=True)  11.7 us
    reduce_sum x1, other arithmetic, body(): jnp.sum(points * points, axis=1, keepdims=True) + EPS  4.15 us
    gather x1, local copies, waits for them, and re-layouts, body(): mine = jnp.take(unit, position, axis=0) * valid[:, None].astype(jnp.float32)  4.02 us
    mul x1, other arithmetic, body(): points * lax.rsqrt(jnp.sum(points * points, axis=1, keepdims=True) + EPS)  3.83 us
  transfers between devices with their start and end apart: 1, of which 1 were waited for; matrix products, arithmetic and copies ran while one was open for 0% of the time, Pallas kernels for 0%

profile of v1, /device:TPU:0, one launch (start us, length us, event | category | flops | bytes accessed | tf_op | source)
XLA Modules:
  0.0 147.7 jit_solution(15266913729782118390)
XLA Ops:
  7.2 0.0 all-gather.3.cloned.1.call-start
  7.2 0.7 convert_compare_fusion
  7.9 0.3 reduce-window.9
  8.2 0.1 slice.13
  8.3 0.1 slice_reduce_fusion
  8.5 0.1 add_bitcast_fusion
  8.5 0.1 convert_reduce_fusion.1
  8.7 4.1 %multiply_reduce_fusion = f32[2048]{0:T(1024)S(1)} fusion(f32[2048,1024]{1,0:T(8,128)} %param.3), kind=kLoop, calls=%fused_computation.1 | loop fusion | flops 4192256 | bytes 8396800 | tf_op jit(solution)/shard_map/reduce_sum | solution.py:45
  12.9 1.2 copy-done
  14.1 3.8 %broadcast_multiply_fusion = f32[2048,1024]{1,0:T(8,128)} fusion(f32[2048,1024]{1,0:T(8,128)S(1)} %copy-done, f32[2048]{0:T(1024)S(1)} %add_rsqrt_fusion), kind=kLoop, calls=%fused_computation.3 | loop fusion | flops 2097152 | bytes 16785408 | tf_op jit(solution)/shard_map/mul | solution.py:45
  17.9 4.0 %gather_fusion = f32[24,1024]{1,0:T(8,128)S(1)} fusion(f32[2048,1024]{1,0:T(8,128)} %broadcast_multiply_fusion, s32[1024]{0:T(1024)S(1)} %pad_clamp_fusion), kind=kCustom, calls=%fused_computation | custom fusion | bytes 196704 | tf_op jit(solution)/shard_map/jit(_take)/gather | solution.py:57
  22.0 0.1 select_multiply_fusion
  22.0 11.7 %all_gather.12 = f32[96,1024]{1,0:T(8,128)} all-gather(f32[24,1024]{1,0:T(8,128)S(1)} %select_multiply_fusion), channel_id=1, replica_groups=mesh['pts'=4,'med'=8] {'pts'}, dimensions={0}, use_global_device_ids=true | all-gather | bytes 491520 | tf_op jit(solution)/shard_map/all_gather | solution.py:61
  33.8 0.0 all-gather.3.cloned.1.call-update
  33.8 0.1 convert_reduce_fusion
  34.0 0.1 select_reduce_fusion
  34.1 0.0 copy-start.1
  34.1 38.3 %all-gather.3.cloned.1.call-done = f32[768,1024]{1,0:T(8,128)} async-done(((f32[96,1024]{1,0:T(8,128)}), f32[768,1024]{1,0:T(8,128)}) %all-gather.3.cloned.1.call-update) | async-done | bytes 3145744 | tf_op jit(solution)/shard_map/all_gather | solution.py:63
  72.4 23.3 %add_reduce_fusion = f32[2048]{0:T(1024)S(1)} fusion(f32[2048,1024]{1,0:T(8,128)} %broadcast_multiply_fusion, f32[768,1024]{1,0:T(8,128)} %all-gather.3.cloned.1.call-done, f32[768]{0:T(1024)S(1)} %fusion.14), kind=kOutput, calls=%fused_computation.2 | convolution fusion | flops 19330496512 | bytes 11545600 | tf_op jit(solution)/shard_map/dot_general | solution.py:16
  95.7 1.3 multiply_reduce_fusion.1
  97.0 1.5 %maximum_dynamic-update-slice_fusion = f32[64]{0:T(128)S(1)} fusion(f32[64]{0:T(128)S(1)} %broadcast.176, u32[]{:T(128)S(6)} %multiply.1, f32[1]{0:T(128)} %bitcast.5, f32[1]{0:T(128)} %bitcast.4), kind=kLoop, calls=%fused_computation.57 | loop fusion | flops 2 | bytes 268
  98.5 39.2 %all-reduce = f32[64]{0:T(128)S(1)} all-reduce(f32[64]{0:T(128)S(1)} %maximum_dynamic-update-slice_fusion), channel_id=2, replica_groups=mesh['pts'=4,'med'=8] {'pts','med'}, use_global_device_ids=true, to_apply=%add | all-reduce | flops 64 | bytes 512
  137.6 0.1 reshape.121
  137.7 0.6 fusion.18
  (15 shorter events, 0.2 us)
Async XLA Ops:
  7.2 65.3 %all-gather.3.cloned.1.call-start = ((), (), s32[]{:S(2)}) async-start(), calls=%async_computation | async-start | bytes 3538944 | tf_op jit(solution)/shard_map/all_gather | solution.py:63
  8.3 5.8 %copy-start = (f32[2048,1024]{1,0:T(8,128)S(1)}, f32[2048,1024]{1,0:T(8,128)}, u32[]{:S(2)}) copy-start(f32[2048,1024]{1,0:T(8,128)} %param.3) | copy-start | bytes 25165828
  14.1 19.7 %copy-start.2 = (s32[512]{0:T(512)S(1)}, s32[512]{0:T(512)}, u32[]{:S(2)}) copy-start(s32[512]{0:T(512)} %param.5) | copy-start | bytes 6148
  34.1 61.6 %copy-start.1 = (f32[2048]{0:T(1024)S(1)}, f32[2048]{0:T(1024)}, u32[]{:S(2)}) copy-start(f32[2048]{0:T(1024)} %param.4) | copy-start | bytes 24580
Sparse Core Ops, SparseCore 0:
  33.9 38.4 all-gather.2
